TPU v7x, 128 devices: a 2x2x16 block of a 8x8x16 slice. The times are simulated.
128 devices in a mesh: groups: 4 (over y, x), tp: 16 (over z), blk: 2 (over core).
Axes of the slice: x: 2, y: 2, z: 16, core: 2. Of those that a mesh axis runs over, the one named last changes fastest.
The devices are a block of a 8x8x16 slice.
Arguments:
- tokens: bfloat16 [16384, 7168], P(('groups', 'tp')), parts along dimension 0, may hold values from -6 to 6
- gate_weight: bfloat16 [7168, 2048], P('tp', 'blk'), may hold values from -0.0625 to 0.0625
- up_weight: bfloat16 [7168, 2048], P('tp', 'blk'), may hold values from -0.0625 to 0.0625
- down_weight: bfloat16 [2048, 7168], P('blk', 'tp'), may hold values from -0.125 to 0.125
Outputs:
- mixed: bfloat16 [16384, 7168], P(('groups', 'blk'), 'tp'), parts along dimension 0
There are 4 independent parts, one for each index of `groups`. A program takes and returns all parts, laid end to end along the dimension named above; an argument that names none is the same for every part. Nothing has to cross between parts.
All inputs are finite; a program needn't handle non-finite values.
Results may differ from a plain program's by a relative error of at most 0.005.
Values may be sent and summed in bfloat16 or wider, within the bound.
A program may use at most 128 MiB of HBM per device.

v0:
```python
import jax
import jax.numpy as jnp
from jax import lax
from jax.sharding import PartitionSpec as P


def copy_for_each(value, axis):
    count = lax.axis_size(axis)
    return lax.all_to_all(
        jnp.broadcast_to(value[None], (count, *value.shape)), axis, 0, 0, tiled=True
    )


def joined_along(blocks, dim):
    blocks = jnp.moveaxis(blocks, 0, dim)
    dims = blocks.shape
    return blocks.reshape(*dims[:dim], dims[dim] * dims[dim + 1], *dims[dim + 2 :])


def collect(value, axis, dim):
    blocks = copy_for_each(value, axis)
    return joined_along(blocks, dim)


def local(tokens, gate_weight, up_weight, down_weight):
    gate_part = jnp.dot(
        tokens,
        lax.all_gather(gate_weight, "tp", axis=0, tiled=True),
        preferred_element_type=jnp.float32,
    )
    up_part = jnp.dot(
        tokens,
        lax.all_gather(up_weight, "tp", axis=0, tiled=True),
        preferred_element_type=jnp.float32,
    )
    hidden = (jax.nn.silu(gate_part) * up_part).astype(jnp.bfloat16)
    gathered = lax.all_gather(hidden, "tp", axis=0, tiled=True)
    own_units = lax.all_to_all(gathered, "blk", split_axis=0, concat_axis=1, tiled=True)
    down_full = collect(down_weight, "blk", 0)
    result = jnp.dot(own_units, down_full, preferred_element_type=jnp.float32)
    return result.astype(jnp.bfloat16)


def solution(mesh):
    return jax.shard_map(
        local,
        mesh=mesh,
        in_specs=(P(("groups", "tp"), None), P("tp", "blk"), P("tp", "blk"), P("blk", "tp")),
        out_specs=P(("groups", "blk"), "tp"),
        check_vma=False,
    )
```

profile of v0, /device:TPU:69, one launch (start us, length us, event | category | flops | bytes accessed | tf_op | source)
XLA Modules:
  0.0 482.2 jit_solution(5200594511048581085)
XLA Ops:
  6.5 0.0 all-gather.4.cloned.1.call-start
  6.6 0.7 all-gather.4.cloned.1.call-update
  7.3 0.1 all-gather.6.cloned.1.call-start
  7.4 0.7 all-gather.6.cloned.1.call-update
  8.1 0.1 all-gather.8.cloned.1.call-start
  8.2 173.0 %all-gather.4.cloned.1.call-done = bf16[7168,1024]{1,0:T(8,128)(2,1)} async-done(((bf16[448,1024]{1,0:T(8,128)(2,1)}), bf16[7168,1024]{1,0:T(8,128)(2,1)}) %all-gather.4.cloned.1.call-update) | async-done | bytes 14680080 | tf_op jit(solution)/shard_map/all_gather | solution.py:28
  181.2 8.4 %fusion.5 = f32[256,1024]{1,0:T(8,128)S(1)} fusion(bf16[256,7168]{1,0:T(8,128)(2,1)} %param.4, bf16[7168,1024]{1,0:T(8,128)(2,1)} %all-gather.4.cloned.1.call-done), kind=kOutput, calls=%fused_computation.5 | convolution fusion | flops 3758096384 | bytes 19398656 | tf_op jit(solution)/shard_map/dot_general | solution.py:26
  189.6 0.0 copy-start
  189.6 156.7 %all-gather.6.cloned.1.call-done = bf16[7168,1024]{1,0:T(8,128)(2,1)} async-done(((bf16[448,1024]{1,0:T(8,128)(2,1)}), bf16[7168,1024]{1,0:T(8,128)(2,1)}) %all-gather.6.cloned.1.call-update) | async-done | bytes 14680080 | tf_op jit(solution)/shard_map/all_gather | solution.py:33
  346.3 11.1 %fusion.4 = bf16[256,1024]{1,0:T(8,128)(2,1)} fusion(bf16[256,7168]{1,0:T(8,128)(2,1)} %param.4, bf16[7168,1024]{1,0:T(8,128)(2,1)} %all-gather.6.cloned.1.call-done, f32[256,1024]{1,0:T(8,128)S(1)} %fusion.5), kind=kOutput, calls=%fused_computation.4 | convolution fusion | flops 3759669248 | bytes 19922944 | tf_op jit(solution)/shard_map/dot_general | solution.py:31
  357.4 0.1 all-gather.8.cloned.1.call-update
  357.5 0.0 copy-done
  357.5 0.2 broadcast_in_dim.2
  357.7 5.7 %all_to_all.21 = bf16[2,1024,448]{1,2,0:T(8,128)(2,1)S(1)} all-to-all(bf16[2,1024,448]{1,2,0:T(8,128)(2,1)S(1)} %broadcast_in_dim.2), channel_id=1, replica_groups=mesh['groups'=4,'tp'=16,'blk'=2] {'blk'}, dimensions={0} | all-to-all | bytes 3670016 | tf_op jit(solution)/shard_map/all_to_all | solution.py:9
  363.4 94.5 %all-gather.8.cloned.1.call-done = bf16[4096,1024]{1,0:T(8,128)(2,1)} async-done(((bf16[256,1024]{1,0:T(8,128)(2,1)}), bf16[4096,1024]{1,0:T(8,128)(2,1)}) %all-gather.8.cloned.1.call-update) | async-done | bytes 8388624 | tf_op jit(solution)/shard_map/all_gather | solution.py:37
  457.9 12.6 %all_to_all.22 = bf16[2,2048,1024]{2,1,0:T(8,128)(2,1)S(1)} all-to-all(bf16[2,2048,1024]{2,1,0:T(8,128)(2,1)} %bitcast.13), channel_id=1, replica_groups=mesh['groups'=4,'tp'=16,'blk'=2] {'blk'}, dimensions={0} | all-to-all | bytes 16777216 | tf_op jit(solution)/shard_map/all_to_all | solution.py:38
  470.5 5.1 %bitcast_convert_fusion = bf16[2048,448]{0,1:T(8,128)(2,1)} fusion(bf16[2,1024,448]{1,2,0:T(8,128)(2,1)S(1)} %all_to_all.21, bf16[2,2048,1024]{2,1,0:T(8,128)(2,1)S(1)} %all_to_all.22), kind=kOutput, calls=%fused_computation.2 | convolution fusion | flops 3759013888 | bytes 12058624 | tf_op jit(solution)/shard_map/dot_general | solution.py:40
Async XLA Ops:
  6.5 174.6 %all-gather.4.cloned.1.call-start = ((), (), s32[]{:S(2)}) async-start(), calls=%async_computation.2 | async-start | bytes 15597568 | tf_op jit(solution)/shard_map/all_gather | solution.py:28
  7.3 339.0 %all-gather.6.cloned.1.call-start = ((), (), s32[]{:S(2)}) async-start(), calls=%async_computation.3 | async-start | bytes 15597568 | tf_op jit(solution)/shard_map/all_gather | solution.py:33
  8.1 449.8 %all-gather.8.cloned.1.call-start = ((), (), s32[]{:S(2)}) async-start(), calls=%async_computation.4 | async-start | bytes 8912896 | tf_op jit(solution)/shard_map/all_gather | solution.py:37
  189.6 167.9 %copy-start = (bf16[1024,448]{0,1:T(8,128)(2,1)S(1)}, bf16[1024,448]{0,1:T(8,128)(2,1)}, u32[]{:S(2)}) copy-start(bf16[1024,448]{0,1:T(8,128)(2,1)} %param.7) | copy-start | bytes 2752516
Sparse Core Ops, SparseCore 0:
  9.0 172.1 all-gather.3
  182.8 163.4 all-gather.5
  357.6 100.2 all-gather.7
where the time goes:
time: 482 us
  waiting for transfers between devices  426 us (88%)
  matrix products  24.7 us (5%)
  blocking collectives  18.3 us (4%)
  between operations  13.2 us (3%)
    all_gather x1, waiting for transfers between devices, local(): lax.all_gather(gate_weight, 'tp', axis=0, tiled=True)  173 us
    all_gather x1, waiting for transfers between devices, local(): lax.all_gather(up_weight, 'tp', axis=0, tiled=True)  157 us
    all_gather x1, waiting for transfers between devices, local(): gathered = lax.all_gather(hidden, 'tp', axis=0, tiled=True)  94.5 us
    all_to_all x1, blocking collectives, local(): lax.all_to_all(gathered, 'blk', split_axis=0, concat_axis=1, tiled=True)  12.6 us
    dot_general x1, matrix products, local(): jnp.dot(tokens, lax.all_gather(up_weight, 'tp', axis=0, tiled=True), pref...  11.1 us
  transfers between devices with their start and end apart: 3, of which 3 were waited for; matrix products, arithmetic and copies ran while one was open for 2% of the time, Pallas kernels for 0%

commit v1 on v0

v1 whole, which is shorter than its diff:
```python
import math

import jax
import jax.numpy as jnp
from jax import lax
from jax.sharding import PartitionSpec as P


def quads_of(groups):
    side = math.isqrt(groups)
    return [
        [y * side + x, y * side + x + 1, (y + 1) * side + x, (y + 1) * side + x + 1]
        for y in range(0, side, 2)
        for x in range(0, side, 2)
    ]


def local(groups, tokens, gate_weight, up_weight, down_weight):
    quads = quads_of(groups)
    side = math.isqrt(groups)
    g = lax.axis_index("groups")
    place = (g // side) % 2 * 2 + g % 2
    width = gate_weight.shape[1] // 4
    own = jnp.concatenate(
        [
            lax.dynamic_slice_in_dim(gate_weight, place * width, width, 1),
            lax.dynamic_slice_in_dim(up_weight, place * width, width, 1),
        ],
        axis=1,
    )
    weights = lax.all_gather(own, "tp", axis=0, tiled=True)
    rows = lax.all_gather(tokens, "groups", axis=0, tiled=True, axis_index_groups=quads)
    both = jnp.dot(rows, weights, preferred_element_type=jnp.float32)
    hidden = (jax.nn.silu(both[:, :width]) * both[:, width:]).astype(jnp.bfloat16)
    hidden = lax.all_to_all(
        hidden, "groups", split_axis=0, concat_axis=1, tiled=True, axis_index_groups=quads
    )
    gathered = lax.all_gather(hidden, "tp", axis=0, tiled=True)
    own_units = lax.all_to_all(gathered, "blk", split_axis=0, concat_axis=1, tiled=True)
    down_full = lax.all_gather(down_weight, "blk", axis=0, tiled=True)
    result = jnp.dot(own_units, down_full, preferred_element_type=jnp.float32)
    return result.astype(jnp.bfloat16)


def solution(mesh):
    groups = mesh.shape["groups"]
    return jax.shard_map(
        lambda *a: local(groups, *a),
        mesh=mesh,
        in_specs=(P(("groups", "tp"), None), P("tp", "blk"), P("tp", "blk"), P("blk", "tp")),
        out_specs=P(("groups", "blk"), "tp"),
        check_vma=False,
    )
```

time: 482 us -> 451 us (0.936)
  waiting for transfers between devices: 426 us -> 377 us
  starting transfers between devices: 0.12 us -> 17.6 us
  local copies, waits for them, and re-layouts: 0.22 us -> 9.4 us
  blocking collectives: 18.3 us -> 10.4 us
    all_gather x2 -> x3, waiting for transfers between devices: 330 us -> 253 us  [the longest x1 155 us: local(): lax.all_gather(tokens, 'groups', axis=0, tiled=True, axis_index_groups=qu...]
    all_gather x1, waiting for transfers between devices: 94.5 us -> 116 us  [local(): gathered = lax.all_gather(hidden, 'tp', axis=0, tiled=True)]
    all_to_all x0 -> x1, starting transfers between devices: none -> 17.4 us  [local(): lax.all_to_all(gathered, 'blk', split_axis=0, concat_axis=1, tiled=True)]
    all_to_all x0 -> x2, local copies, waits for them, and re-layouts: none -> 8.32 us  [the longest x1 8.28 us: local(): lax.all_to_all(gathered, 'blk', split_axis=0, concat_axis=1, tiled=True)]
    all_to_all x2 -> x1, blocking collectives: 18.3 us -> 10.4 us  [local(): lax.all_to_all(hidden, 'groups', split_axis=0, concat_axis=1, tiled=True,...]
    all_to_all x0 -> x1, waiting for transfers between devices: none -> 7.13 us  [local(): lax.all_to_all(gathered, 'blk', split_axis=0, concat_axis=1, tiled=True)]
    dot_general x2 -> x1, matrix products: 19.5 us -> 13.2 us  [local(): both = jnp.dot(rows, weights, preferred_element_type=jnp.float32)]
  transfers between devices with their start and end apart: 3 -> 5, of which waited for: 3 -> 4; matrix products, arithmetic and copies ran while one was open for 2% -> 2% of each run, Pallas kernels for 0% -> 0%
where the time goes in v1:
time: 451 us
  waiting for transfers between devices  377 us (84%)
  matrix products  22.3 us (5%)
  starting transfers between devices  17.6 us (4%)
  between operations  13.2 us (3%)
  blocking collectives  10.4 us (2%)
  local copies, waits for them, and re-layouts  9.4 us (2%)
    all_gather x1, waiting for transfers between devices, local(): lax.all_gather(tokens, 'groups', axis=0, tiled=True, axis_index_groups=qu...  155 us
    all_gather x1, waiting for transfers between devices, local(): gathered = lax.all_gather(hidden, 'tp', axis=0, tiled=True)  116 us
    all_gather x1, waiting for transfers between devices, local(): weights = lax.all_gather(own, 'tp', axis=0, tiled=True)  98.1 us
    all_to_all x1, starting transfers between devices, local(): lax.all_to_all(gathered, 'blk', split_axis=0, concat_axis=1, tiled=True)  17.4 us
    dot_general x1, matrix products, local(): both = jnp.dot(rows, weights, preferred_element_type=jnp.float32)  13.2 us
    all_to_all x1, blocking collectives, local(): lax.all_to_all(hidden, 'groups', split_axis=0, concat_axis=1, tiled=True,...  10.4 us
    dot_general x1, matrix products, local(): result = jnp.dot(own_units, down_full, preferred_element_type=jnp.float32)  9.13 us
  transfers between devices with their start and end apart: 5, of which 4 were waited for; matrix products, arithmetic and copies ran while one was open for 2% of the time, Pallas kernels for 0%

profile of v1, /device:TPU:69, one launch (start us, length us, event | category | flops | bytes accessed | tf_op | source)
XLA Modules:
  0.0 450.8 jit_solution(9082602229982257203)
XLA Ops:
  6.5 0.0 all-gather.5.cloned.1.call-start
  6.6 1.1 constant_dynamic-slice_fusion
  7.6 0.8 pad_maximum_fusion
  8.4 0.1 all-gather.5.cloned.1.call-update
  8.5 0.1 all-gather.7.cloned.1.call-start
  8.6 0.7 all-gather.7.cloned.1.call-update
  9.3 0.1 all-gather.9.cloned.1.call-start
  9.4 98.1 %all-gather.5.cloned.1.call-done = bf16[7168,512]{1,0:T(8,128)(2,1)} async-done(((bf16[448,512]{1,0:T(8,128)(2,1)}), bf16[7168,512]{1,0:T(8,128)(2,1)}) %all-gather.5.cloned.1.call-update) | async-done | bytes 7340048 | tf_op jit(solution)/shard_map/all_gather | solution.py:31
  107.4 154.6 %all-gather.7.cloned.1.call-done = bf16[1024,7168]{1,0:T(8,128)(2,1)} async-done(((bf16[256,7168]{1,0:T(8,128)(2,1)}), bf16[1024,7168]{1,0:T(8,128)(2,1)}) %all-gather.7.cloned.1.call-update) | async-done | bytes 14680080 | tf_op jit(solution)/shard_map/all_gather | solution.py:32
  262.0 13.2 %convolution_bitcast_fusion = f32[1024,512]{0,1:T(8,128)S(1)} fusion(bf16[7168,512]{1,0:T(8,128)(2,1)} %all-gather.5.cloned.1.call-done, bf16[1024,7168]{1,0:T(8,128)(2,1)} %all-gather.7.cloned.1.call-done), kind=kOutput, calls=%fused_computation.2 | convolution fusion | flops 7516192768 | bytes 24117248 | tf_op jit(solution)/shard_map/dot_general | solution.py:33
  275.2 0.3 fusion
  275.6 10.4 %all_to_all.38 = bf16[4,256,256]{1,2,0:T(8,128)(2,1)} all-to-all(bf16[4,256,256]{1,2,0:T(8,128)(2,1)S(1)} %bitcast.24), channel_id=1, replica_groups={{0,32,64,96},{1,33,65,97},{2,34,66,98},{3,35,67,99},{4,36,68,100},{5,37..., dimensions={0} | all-to-all | bytes 1048576 | tf_op jit(solution)/shard_map/all_to_all | solution.py:35
  285.9 0.1 all-gather.9.cloned.1.call-update
  286.0 0.1 all-gather.11.cloned.1.call-start
  286.1 0.6 all-gather.11.cloned.1.call-update
  286.6 115.7 %all-gather.9.cloned.1.call-done = bf16[4096,1024]{0,1:T(8,128)(2,1)} async-done(((bf16[256,1024]{0,1:T(8,128)(2,1)}), bf16[4096,1024]{0,1:T(8,128)(2,1)}) %all-gather.9.cloned.1.call-update) | async-done | bytes 8388624 | tf_op jit(solution)/shard_map/all_gather | solution.py:38
  402.3 8.3 %copy.11 = bf16[128,2,8,2048]{3,2,0,1:T(8,128)(2,1)} copy(bf16[128,2,8,2048]{3,2,1,0:T(8,128)(2,1)} %bitcast.21) | data formatting | bytes 16777216 | tf_op jit(solution)/shard_map/all_to_all | solution.py:39
  410.6 17.4 %all-to-all-start.1 = ((bf16[2,2048,1024]{1,2,0:T(8,128)(2,1)}), bf16[2,2048,1024]{1,2,0:T(8,128)(2,1)}, u32[]{:S(2)}, u32[]{:S(2)}) async-start(bf16[2,2048,1024]{1,2,0:T(8,128)(2,1)} %bitcast.20), calls=%async_computation.1 | async-start | bytes 16777216 | tf_op jit(solution)/shard_map/all_to_all | solution.py:39
  428.0 0.0 all-gather.11.cloned.1.call-done
  428.0 7.1 %all-to-all-done.1 = bf16[2,2048,1024]{1,2,0:T(8,128)(2,1)} async-done(((bf16[2,2048,1024]{1,2,0:T(8,128)(2,1)}), bf16[2,2048,1024]{1,2,0:T(8,128)(2,1)}, u32[]{:S(2)}, u32[]{:S(2)}) %all-to-all-start.1) | async-done | bytes 8388640 | tf_op jit(solution)/shard_map/all_to_all | solution.py:39
  435.2 9.1 %convolution_convert_fusion = bf16[2048,448]{0,1:T(8,128)(2,1)} fusion(bf16[2048,448]{0,1:T(8,128)(2,1)} %all-gather.11.cloned.1.call-done, bf16[2048,2048]{0,1:T(8,128)(2,1)} %bitcast.4), kind=kOutput, calls=%fused_computation.1 | convolution fusion | flops 3759013888 | bytes 12058624 | tf_op jit(solution)/shard_map/dot_general | solution.py:41
  (1 shorter events, 0.0 us)
Async XLA Ops:
  6.5 100.9 %all-gather.5.cloned.1.call-start = ((), (), s32[]{:S(2)}) async-start(), calls=%async_computation.2 | async-start | bytes 7798784 | tf_op jit(solution)/shard_map/all_gather | solution.py:31
  8.5 253.5 %all-gather.7.cloned.1.call-start = ((), (), s32[]{:S(2)}) async-start(), calls=%async_computation.3 | async-start | bytes 18350080 | tf_op jit(solution)/shard_map/all_gather | solution.py:32
  9.3 393.0 %all-gather.9.cloned.1.call-start = ((), (), s32[]{:S(2)}) async-start(), calls=%async_computation.4 | async-start | bytes 8912896 | tf_op jit(solution)/shard_map/all_gather | solution.py:38
  286.0 142.1 %all-gather.11.cloned.1.call-start = ((), (), s32[]{:S(2)}) async-start(), calls=%async_computation.5 | async-start | bytes 2752512 | tf_op jit(solution)/shard_map/all_gather | solution.py:40
  410.6 24.6 %all-to-all-start.1 = ((bf16[2,2048,1024]{1,2,0:T(8,128)(2,1)}), bf16[2,2048,1024]{1,2,0:T(8,128)(2,1)}, u32[]{:S(2)}, u32[]{:S(2)}) async-start(bf16[2,2048,1024]{1,2,0:T(8,128)(2,1)} %bitcast.20), calls=%async_computation.1 | async-start | bytes 16777216 | tf_op jit(solution)/shard_map/all_to_all | solution.py:39
Sparse Core Ops, SparseCore 0:
  9.0 98.3 all-gather.4
  109.5 152.4 all-gather.6
  286.1 116.1 all-gather.8
  403.9 23.7 all-gather.10

commit v2 on v0

v2 whole, which is shorter than its diff:
```python
import functools
import math

import jax
import jax.numpy as jnp
from jax import lax
from jax.experimental import pallas as pl
from jax.experimental.pallas import tpu as pltpu
from jax.sharding import PartitionSpec as P

MESH = pl.DeviceIdType.MESH
UNITS = 128


def kernel(side, n, tokens, gate, up, down, out, x, w, hid, peer, made, down_v, result,
           load_sem, w_send, w_recv, x_send, x_recv, xp_send, xp_recv, q_send, q_recv,
           h_send, h_recv, p_send, p_recv, d_send, d_recv, out_sem):
    last = n // 2
    rows, width = tokens.shape
    depth = gate.shape[0]
    half = down.shape[0] // 2
    piece = rows // 4

    g = lax.axis_index("groups")
    z = lax.axis_index("tp")
    c = lax.axis_index("blk")
    px = lax.rem(lax.rem(g, side), 2)
    py = lax.rem(lax.div(g, side), 2)
    place = 2 * py + px
    gx = g + 1 - 2 * px
    gy = g + side * (1 - 2 * py)
    gd = gx + side * (1 - 2 * py)
    mates = (None, gx, gy, gd)
    mate_place = (place, 2 * py + 1 - px, 2 * (1 - py) + px, 2 * (1 - py) + 1 - px)
    ahead, behind = lax.rem(z + 1, n), lax.rem(z + n - 1, n)
    to = (ahead, behind)

    def source(s, d):
        return lax.rem(z + n - s, n) if d == 0 else lax.rem(z + s, n)

    barrier = pltpu.get_barrier_semaphore()
    for target in ({"tp": ahead}, {"tp": behind}, {"groups": gx}, {"groups": gy}, {"groups": gd}, {"blk": 1 - c}):
        pl.semaphore_signal(barrier, inc=1, device_id=target, device_id_type=MESH)
    pl.semaphore_wait(barrier, 6)

    def remote(src, dst, send, recv, target):
        return pltpu.make_async_remote_copy(
            src_ref=src, dst_ref=dst, send_sem=send, recv_sem=recv, device_id=target, device_id_type=MESH
        )

    def w_own(f, u):
        first = pl.multiple_of(f * half + place * UNITS, UNITS)
        return (gate, up)[u].at[:, pl.ds(first, UNITS)]

    def w_at(f, u, block):
        return w.at[f, pl.ds(pl.multiple_of(block * depth, 64), depth), pl.ds(u * UNITS, UNITS)]

    def w_copy(f, s, u, d, block, src=None):
        there = w_at(f, u, block)
        return remote(there if src is None else src, there,
                      w_send.at[f, d, s - 1, u], w_recv.at[f, d, s - 1, u], {"tp": to[d]})

    def w_first(f, u):
        for d in range(2):
            w_copy(f, 1, u, d, z, w_own(f, u)).start()

    def w_step(f, s, stage):
        for u in range(2):
            for d in range(2):
                if stage == "end" and u != d:
                    continue
                block = source(s, d)
                w_copy(f, s, u, d, block).wait_recv()
                if stage == "on" or (stage == "near" and u == d):
                    w_copy(f, s + 1, u, d, block).start()

    def w_steps(f, low, high):
        def body(s, carry):
            w_step(f, s, "on")
            return carry
        lax.fori_loop(low, high, body, 0)

    def x_rows(core, part):
        return pl.ds(pl.multiple_of(core * (2 * piece) + part * piece, piece), piece)

    pieces = ((1, 0, gx), (1, 1, gx), (2, 1, gy), (2, 0, gy), (3, 1, gx), (3, 0, gy))

    def x_copy(i, src):
        slot, part, target = pieces[i]
        return remote(src, x.at[slot, x_rows(c, part)], x_send.at[i], x_recv.at[i], {"groups": target})

    def x_mine(i):
        slot, part, _ = pieces[i]
        return x.at[slot, x_rows(c, part)]

    def x_own(i):
        return tokens.at[x_rows(c, pieces[i][1])]

    def x_pass(i):
        return remote(x_mine(i), x_mine(i), xp_send.at[i], xp_recv.at[i], {"blk": 1 - c})

    def x_pass_in(i):
        slot, part, _ = pieces[i]
        there = x.at[slot, x_rows(1 - c, part)]
        return remote(there, there, xp_send.at[i], xp_recv.at[i], {"blk": 1 - c})

    def lanes(p):
        return pl.ds(pl.multiple_of(p * UNITS, UNITS), UNITS)

    def compute(f, r):
        both = jnp.dot(x[r], w[f], preferred_element_type=jnp.float32)
        a, b = both[:, :UNITS], both[:, UNITS:]
        h = (a / (1.0 + jnp.exp(-a)) * b).astype(jnp.bfloat16)
        if r == 0:
            hid[z, f, :, lanes(place)] = h
        else:
            made[f, r - 1] = h

    def q_copy(f, r):
        return remote(made.at[f, r - 1], hid.at[z, f, :, lanes(place)],
                      q_send.at[f, r - 1], q_recv.at[f, r - 1], {"groups": mates[r]})

    def q_in(f, r):
        there = hid.at[z, f, :, lanes(mate_place[r])]
        return remote(there, there, q_send.at[f, r - 1], q_recv.at[f, r - 1], {"groups": mates[r]})

    def h_copy(f, s, u, d, block):
        there = hid.at[block, f, :, lanes(mate_place[u])]
        return remote(there, there, h_send.at[f, d, s - 1, u], h_recv.at[f, d, s - 1, u], {"tp": to[d]})

    def h_first(f, u):
        for d in range(2):
            h_copy(f, 1, u, d, z).start()

    def h_takes(u, d):
        return u // 2 == d

    def h_step(f, s, stage):
        for u in range(4):
            for d in range(2):
                if stage == "end" and not h_takes(u, d):
                    continue
                block = source(s, d)
                h_copy(f, s, u, d, block).wait_recv()
                if stage == "on" or (stage == "near" and h_takes(u, d)):
                    h_copy(f, s + 1, u, d, block).start()

    def p_copy(f, block):
        at = lax.rem(block, last)
        return remote(hid.at[block, f], peer.at[at, f], p_send.at[at, f], p_recv.at[at, f], {"blk": 1 - c})

    def is_mine(block):
        return lax.div(block, last) == c

    def hand_over(f, block):
        @pl.when(jnp.logical_not(is_mine(block)))
        def _():
            p_copy(f, block).start()

    def out_copy(block):
        at = lax.rem(block, last)
        there = out.at[pl.ds(pl.multiple_of(at * rows, rows), rows)]
        return pltpu.make_async_copy(result.at[at], there, out_sem.at[at])

    def finish(block):
        @pl.when(is_mine(block))
        def _():
            at = lax.rem(block, last)
            p_copy(0, block).wait_recv()
            p_copy(1, block).wait_recv()
            total = jnp.zeros((rows, down.shape[1]), jnp.float32)
            for f in range(2):
                total += jnp.dot(hid[block, f], down_v[0, f * half:(f + 1) * half], preferred_element_type=jnp.float32)
                total += jnp.dot(peer[at, f], down_v[1, f * half:(f + 1) * half], preferred_element_type=jnp.float32)
            result[at] = total.astype(jnp.bfloat16)
            out_copy(block).start()

    w_first(0, 0)
    for i in (0, 2):
        x_copy(i, x_own(i)).start()
    w_first(0, 1)
    for i in (1, 3):
        x_copy(i, x_own(i)).start()
    w_first(1, 0)
    loads = [pltpu.make_async_copy(tokens, x.at[0], load_sem.at[0]),
             pltpu.make_async_copy(down, down_v.at[0], load_sem.at[1])]
    for f in range(2):
        for u in range(2):
            loads.append(pltpu.make_async_copy(w_own(f, u), w_at(f, u, z), load_sem.at[2 + 2 * f + u]))
    for load in loads:
        load.start()
    for load in loads:
        load.wait()
    down_pass = remote(down_v.at[0], down_v.at[1], d_send, d_recv, {"blk": 1 - c})
    down_pass.start()

    w_steps(0, 1, 5)
    for i, fwd in ((0, 5), (2, 4)):
        x_copy(i, x_mine(i)).wait_recv()
        x_copy(fwd, x_mine(i)).start()
        x_pass(i).start()
    w_steps(0, 5, last - 1)
    w_step(0, last - 1, "near")
    w_first(1, 1)
    w_step(1, 1, "on")
    w_step(0, last, "end")
    w_step(1, 2, "on")
    for i in (1, 3):
        x_copy(i, x_mine(i)).wait_recv()
        x_pass(i).start()
    compute(0, 0)
    w_step(1, 3, "on")
    for i in range(4):
        x_pass_in(i).wait_recv()
    compute(0, 1)
    w_step(1, 4, "on")
    q_copy(0, 1).start()
    compute(0, 2)
    w_step(1, 5, "on")
    q_copy(0, 2).start()
    w_step(1, 6, "on")
    for i in (4, 5):
        x_copy(i, x_mine(i)).wait_recv()
        x_pass(i).start()
    w_step(1, last - 1, "near")
    for i in (4, 5):
        x_pass_in(i).wait_recv()
    compute(0, 3)
    h_first(0, 0)
    q_copy(0, 3).start()
    for r in (1, 2, 3):
        q_in(0, r).wait_recv()
        h_first(0, r)
    hand_over(0, z)
    w_step(1, last, "end")

    def h_after(f, s):
        for d in range(2):
            hand_over(f, source(s, d))

    h_step(0, 1, "on")
    h_after(0, 1)
    compute(1, 3)
    compute(1, 1)
    q_copy(1, 3).start()
    h_step(0, 2, "on")
    h_after(0, 2)
    q_copy(1, 1).start()
    compute(1, 2)
    compute(1, 0)
    q_copy(1, 2).start()

    def h0_body(s, carry):
        h_step(0, s, "on")
        h_after(0, s)
        return carry
    lax.fori_loop(3, last - 1, h0_body, 0)
    down_pass.wait()
    h_step(0, last - 1, "near")
    h_after(0, last - 1)
    h_first(1, 0)
    for r in (1, 2, 3):
        q_in(1, r).wait_recv()
        h_first(1, r)
    hand_over(1, z)
    h_step(1, 1, "on")
    h_after(1, 1)
    h_step(0, last, "end")
    hand_over(0, source(last, 0))
    finish(z)

    def h1_body(s, carry):
        h_step(1, s, "on")
        h_after(1, s)
        for d in range(2):
            finish(source(s - 1, d))
        return carry
    lax.fori_loop(2, last - 1, h1_body, 0)
    h_step(1, last - 1, "near")
    h_after(1, last - 1)
    for d in range(2):
        finish(source(last - 2, d))
    h_step(1, last, "end")
    hand_over(1, source(last, 0))
    for d in range(2):
        finish(source(last - 1, d))
    finish(source(last, 0))

    for i in range(6):
        x_copy(i, x_mine(i)).wait_send()
        x_pass(i).wait_send()

    def sent(s, carry):
        for f in range(2):
            for d in range(2):
                for u in range(2):
                    w_copy(f, s, u, d, z).wait_send()
                for u in range(4):
                    h_copy(f, s, u, d, z).wait_send()
        return carry
    lax.fori_loop(1, last, sent, 0)
    for f in range(2):
        for d in range(2):
            w_copy(f, last, d, d, z).wait_send()
            for u in range(4):
                if h_takes(u, d):
                    h_copy(f, last, u, d, z).wait_send()
        for r in (1, 2, 3):
            q_copy(f, r).wait_send()

    def leave(i, carry):
        p_copy(0, (1 - c) * last + i).wait_send()
        p_copy(1, (1 - c) * last + i).wait_send()
        out_copy(i).wait()
        return carry
    lax.fori_loop(0, last, leave, 0)


def solution(mesh):
    n = mesh.shape["tp"]
    side = math.isqrt(mesh.shape["groups"])

    def local(tokens, gate, up, down):
        rows, width = tokens.shape
        last = n // 2
        columns = down.shape[1]
        bf16 = jnp.bfloat16
        dma = pltpu.SemaphoreType.DMA
        return pl.pallas_call(
            functools.partial(kernel, side, n),
            out_shape=jax.ShapeDtypeStruct((rows * last, columns), bf16),
            in_specs=[pl.BlockSpec(memory_space=pl.ANY)] * 4,
            out_specs=pl.BlockSpec(memory_space=pl.ANY),
            scratch_shapes=[
                pltpu.VMEM((4, rows, width), bf16),
                pltpu.VMEM((2, width, 2 * UNITS), bf16),
                pltpu.VMEM((n, 2, rows, 4 * UNITS), bf16),
                pltpu.VMEM((last, 2, rows, 4 * UNITS), bf16),
                pltpu.VMEM((2, 3, rows, UNITS), bf16),
                pltpu.VMEM((2, *down.shape), bf16),
                pltpu.VMEM((last, rows, columns), bf16),
                dma((6,)),
                dma((2, 2, last, 2)), dma((2, 2, last, 2)),
                dma((6,)), dma((6,)), dma((6,)), dma((6,)),
                dma((2, 3)), dma((2, 3)),
                dma((2, 2, last, 4)), dma((2, 2, last, 4)),
                dma((last, 2)), dma((last, 2)),
                dma, dma,
                dma((last,)),
            ],
            compiler_params=pltpu.CompilerParams(
                collective_id=0, has_side_effects=True, vmem_limit_bytes=60 * 2**20
            ),
        )(tokens, gate, up, down)

    return jax.shard_map(
        local,
        mesh=mesh,
        in_specs=(P(("groups", "tp"), None), P("tp", "blk"), P("tp", "blk"), P("blk", "tp")),
        out_specs=P(("groups", "blk"), "tp"),
        check_vma=False,
    )
```

time: 482 us -> 195 us (0.40)
  waiting for transfers between devices: 426 us -> 0 us
  Pallas kernels: 0 us -> 188 us
  matrix products: 24.7 us -> 0 us
  blocking collectives: 18.3 us -> 0 us
  between operations: 13.2 us -> 0.01 us
  local copies, waits for them, and re-layouts: 0.22 us -> 6.1 us
    all_gather x3 -> x0, waiting for transfers between devices: 424 us -> none  [the longest x1 173 us: local(): lax.all_gather(gate_weight, 'tp', axis=0, tiled=True)]
    pallas_call x0 -> x1, Pallas kernels: none -> 188 us  [local(): pl.pallas_call(functools.partial(kernel, side, n), out_shape=jax.ShapeDty...]
    dot_general x3 -> x0, matrix products: 24.7 us -> none  [the longest x1 11.1 us: local(): jnp.dot(tokens, lax.all_gather(up_weight, 'tp', axis=0, tiled=True), pref...]
    all_to_all x2 -> x0, blocking collectives: 18.3 us -> none  [the longest x1 12.6 us: local(): lax.all_to_all(gathered, 'blk', split_axis=0, concat_axis=1, tiled=True)]
  transfers between devices with their start and end apart: 3 -> 0, of which waited for: 3 -> 0; matrix products, arithmetic and copies ran while one was open for 2% -> 0% of each run, Pallas kernels for 0% -> 0%
where the time goes in v2:
time: 195 us
  Pallas kernels  188 us (96%)
  local copies, waits for them, and re-layouts  6.1 us (3%)
    pallas_call x1, Pallas kernels, local(): pl.pallas_call(functools.partial(kernel, side, n), out_shape=jax.ShapeDty...  188 us

profile of v2, /device:TPU:69, one launch (start us, length us, event | category | flops | bytes accessed | tf_op | source)
XLA Modules:
  0.0 194.5 jit_solution(10150238618969893834)
XLA Ops:
  0.0 2.2 %copy.5.down = bf16[1024,448]{1,0:T(8,128)(2,1)} copy(bf16[1024,448]{0,1:T(8,128)(2,1)} %param.7) | data formatting | bytes 1835008 | tf_op args[3]
  2.2 188.4 %shard_map.46 = bf16[2048,448]{1,0:T(8,128)(2,1)} custom-call(bf16[256,7168]{1,0:T(8,128)(2,1)} %tokens.1, bf16[448,1024]{1,0:T(8,128)(2,1)} %gate.1, bf16[448,1024]{1,0:T(8,128)(2,1)} %up.1, bf16[1024,448]{1,0:T(8,128)(2,1)} %copy.5.down), custom_call_target="tpu_custom_call" | custom-call | tf_op jit(solution)/shard_map/pallas_call | solution.py:329
  190.7 3.9 %copy.6 = bf16[2048,448]{0,1:T(8,128)(2,1)} copy(bf16[2048,448]{1,0:T(8,128)(2,1)} %shard_map.46) | data formatting | bytes 3670016 | tf_op jit(solution)/shard_map/pallas_call | solution.py:329

commit v3 on v2

v3 whole, which is shorter than its diff:
```python
import functools
import math

import jax
import jax.numpy as jnp
from jax import lax
from jax.experimental import pallas as pl
from jax.experimental.pallas import tpu as pltpu
from jax.sharding import PartitionSpec as P

MESH = pl.DeviceIdType.MESH
UNITS = 128
SLOTS = 6


def kernel(side, n, tokens, gate, up, down, out, x, w, hid, peer, made, down_v, partial, result,
           load_sem, early, arrived, w_send, x_send, x_recv, xp_send, xp_recv, q_send, q_recv,
           h_send, p_send, p_recv, rest, d_send, d_recv, out_sem):
    last = n // 2
    rows, width = tokens.shape
    depth = gate.shape[0]
    half = gate.shape[1] // 2
    piece = rows // 4

    g = lax.axis_index("groups")
    z = lax.axis_index("tp")
    c = lax.axis_index("blk")
    px = lax.rem(lax.rem(g, side), 2)
    py = lax.rem(lax.div(g, side), 2)
    place = 2 * py + px
    gx = g + 1 - 2 * px
    gy = g + side * (1 - 2 * py)
    gd = gx + side * (1 - 2 * py)
    mates = (None, gx, gy, gd)
    mate_place = (place, 2 * py + 1 - px, 2 * (1 - py) + px, 2 * (1 - py) + 1 - px)
    ahead, behind = lax.rem(z + 1, n), lax.rem(z + n - 1, n)
    to = (ahead, behind)

    def source(s, d):
        return lax.rem(z + n - s, n) if d == 0 else lax.rem(z + s, n)

    barrier = pltpu.get_barrier_semaphore()
    for target in ({"tp": ahead}, {"tp": behind}, {"groups": gx}, {"groups": gy}, {"groups": gd}, {"blk": 1 - c}):
        pl.semaphore_signal(barrier, inc=1, device_id=target, device_id_type=MESH)
    pl.semaphore_wait(barrier, 6)

    def remote(src, dst, send, recv, target):
        return pltpu.make_async_remote_copy(
            src_ref=src, dst_ref=dst, send_sem=send, recv_sem=recv, device_id=target, device_id_type=MESH
        )

    def arrival(half_of, f, s, u, d):
        if f == 0:
            order = last if isinstance(s, int) and s == last else s - 1
        else:
            order = last - 1 if isinstance(s, int) and s == 1 else s + last - 1
        return arrived.at[lax.rem(2 * last * half_of + order, SLOTS), d, u]

    def w_own(f, u):
        first = pl.multiple_of(f * half + place * UNITS, UNITS)
        return (gate, up)[u].at[:, pl.ds(first, UNITS)]

    def w_at(f, u, block):
        return w.at[f, pl.ds(pl.multiple_of(block * depth, 64), depth), pl.ds(u * UNITS, UNITS)]

    def w_copy(f, s, u, d, block, src=None):
        there = w_at(f, u, block)
        first = f == 1 and u == 0 and isinstance(s, int) and s == 1
        return remote(there if src is None else src, there, w_send.at[f],
                      early.at[d] if first else arrival(0, f, s, u, d), {"tp": to[d]})

    def w_first(f, u):
        for d in range(2):
            w_copy(f, 1, u, d, z, w_own(f, u)).start()

    def w_step(f, s, stage):
        for u in range(2):
            for d in range(2):
                if stage == "end" and u != d:
                    continue
                block = source(s, d)
                w_copy(f, s, u, d, block).wait_recv()
                if stage == "on" or (stage == "near" and u == d):
                    w_copy(f, s + 1, u, d, block).start()

    def w_steps(f, low, high):
        def body(s, carry):
            w_step(f, s, "on")
            return carry
        lax.fori_loop(low, high, body, 0)

    def x_rows(core, part):
        return pl.ds(pl.multiple_of(core * (2 * piece) + part * piece, piece), piece)

    pieces = ((1, 0, gx), (1, 1, gx), (2, 1, gy), (2, 0, gy), (3, 1, gx), (3, 0, gy))

    def x_copy(i, src):
        slot, part, target = pieces[i]
        return remote(src, x.at[slot, x_rows(c, part)], x_send, x_recv.at[i], {"groups": target})

    def x_mine(i):
        slot, part, _ = pieces[i]
        return x.at[slot, x_rows(c, part)]

    def x_own(i):
        return tokens.at[x_rows(c, pieces[i][1])]

    def x_pass(i):
        return remote(x_mine(i), x_mine(i), xp_send, xp_recv.at[i], {"blk": 1 - c})

    def x_pass_in(i):
        slot, part, _ = pieces[i]
        there = x.at[slot, x_rows(1 - c, part)]
        return remote(there, there, xp_send, xp_recv.at[i], {"blk": 1 - c})

    def lanes(f, p):
        return pl.ds(pl.multiple_of(f * half + p * UNITS, UNITS), UNITS)

    def compute(f, r):
        both = jnp.dot(x[r], w[f], preferred_element_type=jnp.float32)
        a, b = both[:, :UNITS], both[:, UNITS:]
        h = (a / (1.0 + jnp.exp(-a)) * b).astype(jnp.bfloat16)
        if r == 0:
            hid[z, :, lanes(f, place)] = h
        else:
            made[f, r - 1] = h

    def q_copy(f, r):
        return remote(made.at[f, r - 1], hid.at[z, :, lanes(f, place)],
                      q_send, q_recv.at[f, r - 1], {"groups": mates[r]})

    def q_in(f, r):
        there = hid.at[z, :, lanes(f, mate_place[r])]
        return remote(there, there, q_send, q_recv.at[f, r - 1], {"groups": mates[r]})

    def h_copy(f, s, u, d, block):
        there = hid.at[block, :, lanes(f, mate_place[u])]
        return remote(there, there, h_send.at[f], arrival(1, f, s, u, d), {"tp": to[d]})

    def h_first(f, u):
        for d in range(2):
            h_copy(f, 1, u, d, z).start()

    def h_takes(u, d):
        return u % 2 == d

    def h_step(f, s, stage):
        for u in range(4):
            for d in range(2):
                if stage == "end" and not h_takes(u, d):
                    continue
                block = source(s, d)
                h_copy(f, s, u, d, block).wait_recv()
                if stage == "on" or (stage == "near" and h_takes(u, d)):
                    h_copy(f, s + 1, u, d, block).start()

    def p_copy(first, wide, block, sem=None):
        at = lax.rem(block, last)
        part = pl.ds(first, wide)
        return remote(hid.at[block, :, part], peer.at[at, :, part], p_send,
                      p_recv.at[at] if sem is None else sem, {"blk": 1 - c})

    def is_mine(block):
        return lax.div(block, last) == c

    def hand_over(f, block):
        @pl.when(jnp.logical_not(is_mine(block)))
        def _():
            p_copy(f * half, half, block).start()

    def times(weight, units):
        return lax.dot_general(weight, units, (((1,), (1,)), ((), ())), preferred_element_type=jnp.float32)

    def put_out(block, total):
        columns = pl.ds(pl.multiple_of(lax.rem(block, last) * rows, rows), rows)
        result[:, columns] = total.astype(jnp.bfloat16)
        pltpu.make_async_copy(result.at[:, columns], out.at[:, columns], out_sem).start()

    def finish(block):
        @pl.when(is_mine(block))
        def _():
            p_copy(0, 2 * half, block).wait_recv()
            put_out(block, times(down_v[0], hid[block]) + times(down_v[1], peer[lax.rem(block, last)]))

    def finish_far():
        block = source(last, 0)
        at = lax.rem(block, last)
        parts = [pl.ds(pl.multiple_of(half + row * 2 * UNITS, 2 * UNITS), 2 * UNITS) for row in (py, 1 - py)]

        def both(part):
            return times(down_v[0, :, part], hid[block, :, part]) + times(down_v[1, :, part], peer[at, :, part])

        for i in range(2):
            for d in range(2):
                h_copy(1, last, 2 * i + d, d, block).wait_recv()
            first = pl.multiple_of(half + (py, 1 - py)[i] * 2 * UNITS, 2 * UNITS)
            sem = None if i == 0 else rest

            @pl.when(jnp.logical_not(is_mine(block)))
            def _():
                p_copy(first, 2 * UNITS, block, sem).start()

            @pl.when(is_mine(block))
            def _():
                if i == 0:
                    p_copy(0, half + 2 * UNITS, block).wait_recv()
                    partial[...] = both(pl.ds(0, half)) + both(parts[0])
                else:
                    p_copy(0, 2 * UNITS, block, rest).wait_recv()
                    put_out(block, partial[...] + both(parts[1]))

    w_first(0, 0)
    for i in (0, 2):
        x_copy(i, x_own(i)).start()
    w_first(0, 1)
    for i in (1, 3):
        x_copy(i, x_own(i)).start()
    w_first(1, 0)
    own_rows = pl.ds(pl.multiple_of(z * depth, 64), depth)
    pltpu.make_async_copy(tokens, x.at[0], load_sem.at[0]).start()
    down_load = pltpu.make_async_copy(down, down_v.at[0], load_sem.at[1])
    down_load.start()
    for f in range(2):
        for u in range(2):
            pltpu.make_async_copy(w_own(f, u), w_at(f, u, z), load_sem.at[2]).start()
    w_steps(0, 1, 5)
    pltpu.make_async_copy(tokens, x.at[0], load_sem.at[0]).wait()
    pltpu.make_async_copy(w.at[:, own_rows], w.at[:, own_rows], load_sem.at[2]).wait()
    down_load.wait()
    down_pass = remote(down_v.at[0], down_v.at[1], d_send, d_recv, {"blk": 1 - c})
    down_pass.start()
    for i, fwd in ((0, 5), (2, 4)):
        x_copy(i, x_mine(i)).wait_recv()
        x_copy(fwd, x_mine(i)).start()
        x_pass(i).start()
    w_steps(0, 5, last - 1)
    w_step(0, last - 1, "near")
    w_first(1, 1)
    w_step(1, 1, "on")
    w_step(0, last, "end")
    w_step(1, 2, "on")
    for i in (1, 3):
        x_copy(i, x_mine(i)).wait_recv()
        x_pass(i).start()
    compute(0, 0)
    w_step(1, 3, "on")
    for i in range(4):
        x_pass_in(i).wait_recv()
    compute(0, 1)
    w_step(1, 4, "on")
    q_copy(0, 1).start()
    compute(0, 2)
    w_step(1, 5, "on")
    q_copy(0, 2).start()
    w_step(1, 6, "on")
    for i in (4, 5):
        x_copy(i, x_mine(i)).wait_recv()
        x_pass(i).start()
    w_step(1, last - 1, "near")
    h_first(0, 0)
    for r in (1, 2):
        q_in(0, r).wait_recv()
        h_first(0, r)
    for i in (4, 5):
        x_pass_in(i).wait_recv()
    compute(0, 3)
    q_copy(0, 3).start()
    q_in(0, 3).wait_recv()
    h_first(0, 3)
    hand_over(0, z)
    w_step(1, last, "end")

    def h_after(f, s):
        for d in range(2):
            hand_over(f, source(s, d))

    h_step(0, 1, "on")
    h_after(0, 1)
    compute(1, 3)
    compute(1, 1)
    q_copy(1, 3).start()
    h_step(0, 2, "on")
    h_after(0, 2)
    q_copy(1, 1).start()
    compute(1, 2)
    compute(1, 0)
    q_copy(1, 2).start()

    def h0_body(s, carry):
        h_step(0, s, "on")
        h_after(0, s)
        return carry
    lax.fori_loop(3, last - 1, h0_body, 0)
    down_pass.wait()
    h_step(0, last - 1, "near")
    h_after(0, last - 1)
    h_first(1, 0)
    for r in (1, 2, 3):
        q_in(1, r).wait_recv()
        h_first(1, r)
    hand_over(1, z)
    h_step(1, 1, "on")
    h_after(1, 1)
    h_step(0, last, "end")
    hand_over(0, source(last, 0))
    finish(z)

    def h1_body(s, carry):
        h_step(1, s, "on")
        h_after(1, s)
        for d in range(2):
            finish(source(s - 1, d))
        return carry
    lax.fori_loop(2, last - 1, h1_body, 0)
    h_step(1, last - 1, "near")
    h_after(1, last - 1)
    for d in range(2):
        finish(source(last - 2, d))
    for d in range(2):
        finish(source(last - 1, d))
    finish_far()

    def left(ref, sem):
        remote(ref, ref, sem, rest, {"blk": 1 - c}).wait_send()

    left(x.at[pl.ds(0, 3), pl.ds(0, 2 * piece)], x_send)
    left(x.at[pl.ds(0, 3), pl.ds(0, 2 * piece)], xp_send)
    for f in range(2):
        left(w.at[f, pl.ds(0, (n - 1) * depth)], w_send.at[f])
        left(hid.at[pl.ds(0, n - 1), :, pl.ds(0, half)], h_send.at[f])
    left(made, q_send)
    left(peer, p_send)
    pltpu.make_async_copy(result, out, out_sem).wait()


def solution(mesh):
    n = mesh.shape["tp"]
    side = math.isqrt(mesh.shape["groups"])

    def local(tokens, gate, up, down):
        down = down.T
        rows, width = tokens.shape
        last = n // 2
        columns = down.shape[0]
        bf16 = jnp.bfloat16
        dma = pltpu.SemaphoreType.DMA
        return pl.pallas_call(
            functools.partial(kernel, side, n),
            out_shape=jax.ShapeDtypeStruct((columns, rows * last), bf16),
            in_specs=[pl.BlockSpec(memory_space=pl.ANY)] * 4,
            out_specs=pl.BlockSpec(memory_space=pl.ANY),
            scratch_shapes=[
                pltpu.VMEM((4, rows, width), bf16),
                pltpu.VMEM((2, width, 2 * UNITS), bf16),
                pltpu.VMEM((n, rows, 8 * UNITS), bf16),
                pltpu.VMEM((last, rows, 8 * UNITS), bf16),
                pltpu.VMEM((2, 3, rows, UNITS), bf16),
                pltpu.VMEM((2, *down.shape), bf16),
                pltpu.VMEM((columns, rows), jnp.float32),
                pltpu.VMEM((columns, rows * last), bf16),
                dma((3,)), dma((2,)), dma((SLOTS, 2, 4)), dma((2,)),
                dma, dma((6,)), dma, dma((6,)),
                dma, dma((2, 3)),
                dma((2,)), dma, dma((last,)), dma,
                dma, dma, dma,
            ],
            compiler_params=pltpu.CompilerParams(
                collective_id=0, has_side_effects=True, vmem_limit_bytes=60 * 2**20
            ),
        )(tokens, gate, up, down).T

    return jax.shard_map(
        local,
        mesh=mesh,
        in_specs=(P(("groups", "tp"), None), P("tp", "blk"), P("tp", "blk"), P("blk", "tp")),
        out_specs=P(("groups", "blk"), "tp"),
        check_vma=False,
    )
```

time: 195 us -> 186 us (0.954)
  Pallas kernels: 188 us -> 183 us
  local copies, waits for them, and re-layouts: 6.1 us -> 2.94 us
    pallas_call x1, Pallas kernels: 188 us -> 183 us  [local(): pl.pallas_call(functools.partial(kernel, side, n), out_shape=jax.ShapeDty...]
    pallas_call x1 -> x0, local copies, waits for them, and re-layouts: 3.86 us -> none  [local(): pl.pallas_call(functools.partial(kernel, side, n), out_shape=jax.ShapeDty...]
where the time goes in v3:
time: 186 us
  Pallas kernels  183 us (98%)
  local copies, waits for them, and re-layouts  2.94 us (2%)
    pallas_call x1, Pallas kernels, local(): pl.pallas_call(functools.partial(kernel, side, n), out_shape=jax.ShapeDty...  183 us

profile of v3, /device:TPU:69, one launch (start us, length us, event | category | flops | bytes accessed | tf_op | source)
XLA Modules:
  0.0 185.9 jit_solution(3918248772573917151)
XLA Ops:
  0.0 182.9 %shard_map.46 = bf16[448,2048]{1,0:T(8,128)(2,1)} custom-call(bf16[256,7168]{1,0:T(8,128)(2,1)} %tokens.1, bf16[448,1024]{1,0:T(8,128)(2,1)} %gate.1, bf16[448,1024]{1,0:T(8,128)(2,1)} %up.1, bf16[448,1024]{1,0:T(8,128)(2,1)} %bitcast.3), custom_call_target="tpu_custom_call" | custom-call | tf_op jit(solution)/shard_map/pallas_call | solution.py:347
  182.9 2.9 %copy.6 = bf16[2048,448]{0,1:T(8,128)(2,1)} copy(bf16[2048,448]{0,1:T(8,128)(2,1)} %bitcast.2) | data formatting | bytes 3670016

commit v4 on v3

--- a/solution.py
+++ b/solution.py
@@ -13,9 +13,9 @@
 SLOTS = 6
 
 
-def kernel(side, n, tokens, gate, up, down, out, x, w, hid, peer, made, down_v, partial, result,
+def kernel(side, n, tokens, gate, up, down, out, x, w, hid, peer, made, down_v, partial,
            load_sem, early, arrived, w_send, x_send, x_recv, xp_send, xp_recv, q_send, q_recv,
-           h_send, p_send, p_recv, rest, d_send, d_recv, out_sem):
+           h_send, p_send, p_recv, rest, d_send, d_recv):
     last = n // 2
     rows, width = tokens.shape
     depth = gate.shape[0]
@@ -49,38 +49,42 @@
             src_ref=src, dst_ref=dst, send_sem=send, recv_sem=recv, device_id=target, device_id_type=MESH
         )
 
-    def arrival(half_of, f, s, u, d):
+    def takes(u, d):
+        return u % 2 == d
+
+    def arrival(stage, f, s, u, d):
+        if isinstance(s, int) and s == 1:
+            return early.at[2 * stage + f, d, u]
         if f == 0:
             order = last if isinstance(s, int) and s == last else s - 1
         else:
-            order = last - 1 if isinstance(s, int) and s == 1 else s + last - 1
-        return arrived.at[lax.rem(2 * last * half_of + order, SLOTS), d, u]
+            order = s + last - 1
+        return arrived.at[lax.rem(2 * last * stage + order, SLOTS), d, u]
 
     def w_own(f, u):
         first = pl.multiple_of(f * half + place * UNITS, UNITS)
-        return (gate, up)[u].at[:, pl.ds(first, UNITS)]
+        return (gate, up)[u % 2].at[pl.ds(u // 2 * (depth // 2), depth // 2), pl.ds(first, UNITS)]
 
     def w_at(f, u, block):
-        return w.at[f, pl.ds(pl.multiple_of(block * depth, 64), depth), pl.ds(u * UNITS, UNITS)]
+        first = pl.multiple_of(block * depth + u // 2 * (depth // 2), 32)
+        return w.at[f, pl.ds(first, depth // 2), pl.ds(u % 2 * UNITS, UNITS)]
 
     def w_copy(f, s, u, d, block, src=None):
         there = w_at(f, u, block)
-        first = f == 1 and u == 0 and isinstance(s, int) and s == 1
-        return remote(there if src is None else src, there, w_send.at[f],
-                      early.at[d] if first else arrival(0, f, s, u, d), {"tp": to[d]})
+        return remote(there if src is None else src, there, w_send.at[f], arrival(0, f, s, u, d), {"tp": to[d]})
 
     def w_first(f, u):
         for d in range(2):
             w_copy(f, 1, u, d, z, w_own(f, u)).start()
 
     def w_step(f, s, stage):
-        for u in range(2):
+        for u in range(4):
             for d in range(2):
-                if stage == "end" and u != d:
+                if stage == "end" and not takes(u, d):
                     continue
                 block = source(s, d)
                 w_copy(f, s, u, d, block).wait_recv()
-                if stage == "on" or (stage == "near" and u == d):
+                if stage == "on" or (stage == "near" and takes(u, d)):
                     w_copy(f, s + 1, u, d, block).start()
 
     def w_steps(f, low, high):
@@ -141,17 +145,14 @@
         for d in range(2):
             h_copy(f, 1, u, d, z).start()
 
-    def h_takes(u, d):
-        return u % 2 == d
-
-    def h_step(f, s, stage):
-        for u in range(4):
+    def h_step(f, s, stage, quarters=range(4)):
+        for u in quarters:
             for d in range(2):
-                if stage == "end" and not h_takes(u, d):
+                if stage == "end" and not takes(u, d):
                     continue
                 block = source(s, d)
                 h_copy(f, s, u, d, block).wait_recv()
-                if stage == "on" or (stage == "near" and h_takes(u, d)):
+                if stage == "on" or (stage == "near" and takes(u, d)):
                     h_copy(f, s + 1, u, d, block).start()
 
     def p_copy(first, wide, block, sem=None):
@@ -173,8 +174,7 @@
 
     def put_out(block, total):
         columns = pl.ds(pl.multiple_of(lax.rem(block, last) * rows, rows), rows)
-        result[:, columns] = total.astype(jnp.bfloat16)
-        pltpu.make_async_copy(result.at[:, columns], out.at[:, columns], out_sem).start()
+        out[:, columns] = total.astype(jnp.bfloat16)
 
     def finish(block):
         @pl.when(is_mine(block))
@@ -210,20 +210,24 @@
                     put_out(block, partial[...] + both(parts[1]))
 
     w_first(0, 0)
+    w_first(0, 1)
     for i in (0, 2):
         x_copy(i, x_own(i)).start()
-    w_first(0, 1)
+    w_first(0, 2)
+    w_first(0, 3)
     for i in (1, 3):
         x_copy(i, x_own(i)).start()
-    w_first(1, 0)
+    for u in range(4):
+        w_first(1, u)
     own_rows = pl.ds(pl.multiple_of(z * depth, 64), depth)
     pltpu.make_async_copy(tokens, x.at[0], load_sem.at[0]).start()
     down_load = pltpu.make_async_copy(down, down_v.at[0], load_sem.at[1])
     down_load.start()
     for f in range(2):
-        for u in range(2):
+        for u in range(4):
             pltpu.make_async_copy(w_own(f, u), w_at(f, u, z), load_sem.at[2]).start()
-    w_steps(0, 1, 5)
+    w_step(0, 1, "on")
+    w_steps(0, 2, 5)
     pltpu.make_async_copy(tokens, x.at[0], load_sem.at[0]).wait()
     pltpu.make_async_copy(w.at[:, own_rows], w.at[:, own_rows], load_sem.at[2]).wait()
     down_load.wait()
@@ -235,36 +239,38 @@
         x_pass(i).start()
     w_steps(0, 5, last - 1)
     w_step(0, last - 1, "near")
-    w_first(1, 1)
     w_step(1, 1, "on")
     w_step(0, last, "end")
-    w_step(1, 2, "on")
+    compute(0, 0)
     for i in (1, 3):
         x_copy(i, x_mine(i)).wait_recv()
         x_pass(i).start()
-    compute(0, 0)
-    w_step(1, 3, "on")
+    h_first(0, 0)
+    w_step(1, 2, "on")
     for i in range(4):
         x_pass_in(i).wait_recv()
     compute(0, 1)
-    w_step(1, 4, "on")
+    w_step(1, 3, "on")
     q_copy(0, 1).start()
     compute(0, 2)
+    w_step(1, 4, "on")
+    q_copy(0, 2).start()
+    q_in(0, 1).wait_recv()
+    h_first(0, 1)
     w_step(1, 5, "on")
-    q_copy(0, 2).start()
-    w_step(1, 6, "on")
     for i in (4, 5):
         x_copy(i, x_mine(i)).wait_recv()
         x_pass(i).start()
-    w_step(1, last - 1, "near")
-    h_first(0, 0)
-    for r in (1, 2):
-        q_in(0, r).wait_recv()
-        h_first(0, r)
+    q_in(0, 2).wait_recv()
+    h_first(0, 2)
+    w_step(1, 6, "on")
     for i in (4, 5):
         x_pass_in(i).wait_recv()
     compute(0, 3)
     q_copy(0, 3).start()
+    h_step(0, 1, "on", (0, 1))
+    w_step(1, last - 1, "near")
+    h_step(0, 1, "on", (2,))
     q_in(0, 3).wait_recv()
     h_first(0, 3)
     hand_over(0, z)
@@ -274,50 +280,44 @@
         for d in range(2):
             hand_over(f, source(s, d))
 
-    h_step(0, 1, "on")
-    h_after(0, 1)
-    compute(1, 3)
-    compute(1, 1)
-    q_copy(1, 3).start()
-    h_step(0, 2, "on")
-    h_after(0, 2)
-    q_copy(1, 1).start()
-    compute(1, 2)
-    compute(1, 0)
-    q_copy(1, 2).start()
-
-    def h0_body(s, carry):
-        h_step(0, s, "on")
+    for s in range(1, 7):
+        h_step(0, s, "on", (3,) if s == 1 else range(4))
         h_after(0, s)
-        return carry
-    lax.fori_loop(3, last - 1, h0_body, 0)
-    down_pass.wait()
-    h_step(0, last - 1, "near")
-    h_after(0, last - 1)
+        if 2 < s < 6:
+            q_copy(1, (3, 1, 2)[s - 3]).start()
+        if 1 < s < 6:
+            compute(1, (3, 1, 2, 0)[s - 2])
     h_first(1, 0)
     for r in (1, 2, 3):
         q_in(1, r).wait_recv()
         h_first(1, r)
     hand_over(1, z)
+    h_step(0, last - 1, "near")
+    h_after(0, last - 1)
+    down_pass.wait()
     h_step(1, 1, "on")
     h_after(1, 1)
     h_step(0, last, "end")
     hand_over(0, source(last, 0))
     finish(z)
+    h_step(1, 2, "on")
+    h_after(1, 2)
+
+    def h1_step(s, stage):
+        h_step(1, s, stage, (0, 1))
+        for d in range(2):
+            finish(source(s - 2, d))
+        h_step(1, s, stage, (2, 3))
+        h_after(1, s)
 
     def h1_body(s, carry):
-        h_step(1, s, "on")
-        h_after(1, s)
-        for d in range(2):
-            finish(source(s - 1, d))
+        h1_step(s, "on")
         return carry
-    lax.fori_loop(2, last - 1, h1_body, 0)
-    h_step(1, last - 1, "near")
-    h_after(1, last - 1)
-    for d in range(2):
-        finish(source(last - 2, d))
-    for d in range(2):
-        finish(source(last - 1, d))
+    lax.fori_loop(3, last - 1, h1_body, 0)
+    h1_step(last - 1, "near")
+    for s in (last - 2, last - 1):
+        for d in range(2):
+            finish(source(s, d))
     finish_far()
 
     def left(ref, sem):
@@ -330,7 +330,6 @@
         left(hid.at[pl.ds(0, n - 1), :, pl.ds(0, half)], h_send.at[f])
     left(made, q_send)
     left(peer, p_send)
-    pltpu.make_async_copy(result, out, out_sem).wait()
 
 
 def solution(mesh):
@@ -347,8 +346,8 @@
         return pl.pallas_call(
             functools.partial(kernel, side, n),
             out_shape=jax.ShapeDtypeStruct((columns, rows * last), bf16),
-            in_specs=[pl.BlockSpec(memory_space=pl.ANY)] * 4,
-            out_specs=pl.BlockSpec(memory_space=pl.ANY),
+            in_specs=[pl.BlockSpec(memory_space=pltpu.HBM)] * 4,
+            out_specs=pl.BlockSpec(memory_space=pltpu.VMEM),
             scratch_shapes=[
                 pltpu.VMEM((4, rows, width), bf16),
                 pltpu.VMEM((2, width, 2 * UNITS), bf16),
@@ -357,17 +356,16 @@
                 pltpu.VMEM((2, 3, rows, UNITS), bf16),
                 pltpu.VMEM((2, *down.shape), bf16),
                 pltpu.VMEM((columns, rows), jnp.float32),
-                pltpu.VMEM((columns, rows * last), bf16),
-                dma((3,)), dma((2,)), dma((SLOTS, 2, 4)), dma((2,)),
+                dma((3,)), dma((4, 2, 4)), dma((SLOTS, 2, 4)), dma((2,)),
                 dma, dma((6,)), dma, dma((6,)),
                 dma, dma((2, 3)),
                 dma((2,)), dma, dma((last,)), dma,
-                dma, dma, dma,
+                dma, dma,
             ],
             compiler_params=pltpu.CompilerParams(
-                collective_id=0, has_side_effects=True, vmem_limit_bytes=60 * 2**20
+                collective_id=0, has_side_effects=True, vmem_limit_bytes=44 * 2**20
             ),
-        )(tokens, gate, up, down).T
+        )(*[pltpu.with_memory_space_constraint(a, pltpu.HBM) for a in (tokens, gate, up, down)]).T
 
     return jax.shard_map(
         local,

time: 186 us -> 184 us (0.989)
  no operation moved by 1% of the time
where the time goes in v4:
time: 184 us
  Pallas kernels  183 us (99%)
    pallas_call x1, Pallas kernels, local(): pl.pallas_call(functools.partial(kernel, side, n), out_shape=jax.ShapeDty...  183 us

profile of v4, /device:TPU:69, one launch (start us, length us, event | category | flops | bytes accessed | tf_op | source)
XLA Modules:
  0.0 183.8 jit_solution(17235777443607708763)
XLA Ops:
  0.0 182.6 %shard_map.46 = bf16[448,2048]{1,0:T(8,128)(2,1)S(1)} custom-call(bf16[256,7168]{1,0:T(8,128)(2,1)} %tokens.1, bf16[448,1024]{1,0:T(8,128)(2,1)} %gate.1, bf16[448,1024]{1,0:T(8,128)(2,1)} %up.1, bf16[448,1024]{1,0:T(8,128)(2,1)} %bitcast.3), custom_call_target="tpu_custom_call" | custom-call | tf_op jit(solution)/shard_map/pallas_call | solution.py:346
  182.6 1.2 copy.6

commit v5 on v4

--- a/solution.py
+++ b/solution.py
@@ -39,11 +39,6 @@
     def source(s, d):
         return lax.rem(z + n - s, n) if d == 0 else lax.rem(z + s, n)
 
-    barrier = pltpu.get_barrier_semaphore()
-    for target in ({"tp": ahead}, {"tp": behind}, {"groups": gx}, {"groups": gy}, {"groups": gd}, {"blk": 1 - c}):
-        pl.semaphore_signal(barrier, inc=1, device_id=target, device_id_type=MESH)
-    pl.semaphore_wait(barrier, 6)
-
     def remote(src, dst, send, recv, target):
         return pltpu.make_async_remote_copy(
             src_ref=src, dst_ref=dst, send_sem=send, recv_sem=recv, device_id=target, device_id_type=MESH
@@ -69,13 +64,13 @@
         first = pl.multiple_of(block * depth + u // 2 * (depth // 2), 32)
         return w.at[f, pl.ds(first, depth // 2), pl.ds(u % 2 * UNITS, UNITS)]
 
-    def w_copy(f, s, u, d, block, src=None):
+    def w_copy(f, s, u, d, block):
         there = w_at(f, u, block)
-        return remote(there if src is None else src, there, w_send.at[f], arrival(0, f, s, u, d), {"tp": to[d]})
+        return remote(there, there, w_send.at[f], arrival(0, f, s, u, d), {"tp": to[d]})
 
     def w_first(f, u):
         for d in range(2):
-            w_copy(f, 1, u, d, z, w_own(f, u)).start()
+            w_copy(f, 1, u, d, z).start()
 
     def w_step(f, s, stage):
         for u in range(4):
@@ -107,7 +102,7 @@
         return x.at[slot, x_rows(c, part)]
 
     def x_own(i):
-        return tokens.at[x_rows(c, pieces[i][1])]
+        return x.at[0, x_rows(c, pieces[i][1])]
 
     def x_pass(i):
         return remote(x_mine(i), x_mine(i), xp_send, xp_recv.at[i], {"blk": 1 - c})
@@ -209,8 +204,27 @@
                     p_copy(0, 2 * UNITS, block, rest).wait_recv()
                     put_out(block, partial[...] + both(parts[1]))
 
-    w_first(0, 0)
-    w_first(0, 1)
+    own_rows = pl.ds(pl.multiple_of(z * depth, 64), depth)
+    for f in range(2):
+        for u in range(4):
+            pltpu.make_async_copy(w_own(f, u), w_at(f, u, z), load_sem.at[f]).start()
+    tokens_load = pltpu.make_async_copy(tokens, x.at[0], load_sem.at[2])
+    tokens_load.start()
+    down_load = pltpu.make_async_copy(down, down_v.at[0], load_sem.at[3])
+    down_load.start()
+
+    barrier = pltpu.get_barrier_semaphore()
+    for target in ({"tp": ahead}, {"tp": behind}, {"groups": gx}, {"groups": gy}, {"groups": gd}, {"blk": 1 - c}):
+        pl.semaphore_signal(barrier, inc=1, device_id=target, device_id_type=MESH)
+    pl.semaphore_wait(barrier, 6)
+
+    for f in range(2):
+        there = w.at[f, own_rows]
+        pltpu.make_async_copy(there, there, load_sem.at[f]).wait()
+        if f == 0:
+            w_first(0, 0)
+            w_first(0, 1)
+    tokens_load.wait()
     for i in (0, 2):
         x_copy(i, x_own(i)).start()
     w_first(0, 2)
@@ -219,17 +233,8 @@
         x_copy(i, x_own(i)).start()
     for u in range(4):
         w_first(1, u)
-    own_rows = pl.ds(pl.multiple_of(z * depth, 64), depth)
-    pltpu.make_async_copy(tokens, x.at[0], load_sem.at[0]).start()
-    down_load = pltpu.make_async_copy(down, down_v.at[0], load_sem.at[1])
-    down_load.start()
-    for f in range(2):
-        for u in range(4):
-            pltpu.make_async_copy(w_own(f, u), w_at(f, u, z), load_sem.at[2]).start()
     w_step(0, 1, "on")
     w_steps(0, 2, 5)
-    pltpu.make_async_copy(tokens, x.at[0], load_sem.at[0]).wait()
-    pltpu.make_async_copy(w.at[:, own_rows], w.at[:, own_rows], load_sem.at[2]).wait()
     down_load.wait()
     down_pass = remote(down_v.at[0], down_v.at[1], d_send, d_recv, {"blk": 1 - c})
     down_pass.start()
@@ -274,25 +279,30 @@
     q_in(0, 3).wait_recv()
     h_first(0, 3)
     hand_over(0, z)
+    h_step(0, 2, "on", (0, 1))
     w_step(1, last, "end")
+    h_step(0, 2, "on", (2,))
 
     def h_after(f, s):
         for d in range(2):
             hand_over(f, source(s, d))
 
-    for s in range(1, 7):
-        h_step(0, s, "on", (3,) if s == 1 else range(4))
-        h_after(0, s)
-        if 2 < s < 6:
-            q_copy(1, (3, 1, 2)[s - 3]).start()
-        if 1 < s < 6:
-            compute(1, (3, 1, 2, 0)[s - 2])
+    h_step(0, 1, "on", (3,))
+    h_after(0, 1)
+    for s in range(3, last):
+        h_step(0, s, "on" if s < last - 1 else "near", range(3))
+        h_step(0, s - 1, "on", (3,))
+        h_after(0, s - 1)
+        if 3 < s < 7:
+            q_copy(1, (3, 1, 2)[s - 4]).start()
+        if s < 7:
+            compute(1, (3, 1, 2, 0)[s - 3])
     h_first(1, 0)
     for r in (1, 2, 3):
         q_in(1, r).wait_recv()
         h_first(1, r)
     hand_over(1, z)
-    h_step(0, last - 1, "near")
+    h_step(0, last - 1, "near", (3,))
     h_after(0, last - 1)
     down_pass.wait()
     h_step(1, 1, "on")
@@ -356,7 +366,7 @@
                 pltpu.VMEM((2, 3, rows, UNITS), bf16),
                 pltpu.VMEM((2, *down.shape), bf16),
                 pltpu.VMEM((columns, rows), jnp.float32),
-                dma((3,)), dma((4, 2, 4)), dma((SLOTS, 2, 4)), dma((2,)),
+                dma((4,)), dma((4, 2, 4)), dma((SLOTS, 2, 4)), dma((2,)),
                 dma, dma((6,)), dma, dma((6,)),
                 dma, dma((2, 3)),
                 dma((2,)), dma, dma((last,)), dma,

time: 184 us -> 182 us (0.989)
  Pallas kernels: 183 us -> 180 us
    pallas_call x1, Pallas kernels: 183 us -> 180 us  [local(): pl.pallas_call(functools.partial(kernel, side, n), out_shape=jax.ShapeDty...]
where the time goes in v5:
time: 182 us; the launch traced here: 181 us
  Pallas kernels  180 us (99%)
    pallas_call x1, Pallas kernels, local(): pl.pallas_call(functools.partial(kernel, side, n), out_shape=jax.ShapeDty...  180 us

profile of v5, /device:TPU:69, one launch (start us, length us, event | category | flops | bytes accessed | tf_op | source)
XLA Modules:
  0.0 181.4 jit_solution(9086288864696726696)
XLA Ops:
  0.0 180.2 %shard_map.46 = bf16[448,2048]{1,0:T(8,128)(2,1)S(1)} custom-call(bf16[256,7168]{1,0:T(8,128)(2,1)} %tokens.1, bf16[448,1024]{1,0:T(8,128)(2,1)} %gate.1, bf16[448,1024]{1,0:T(8,128)(2,1)} %up.1, bf16[448,1024]{1,0:T(8,128)(2,1)} %bitcast.3), custom_call_target="tpu_custom_call" | custom-call | tf_op jit(solution)/shard_map/pallas_call | solution.py:356
  180.2 1.2 copy.6
